TPU v7x, 128 devices: a whole 4x4x4 slice. The times are simulated.
128 devices in a mesh: kv: 64 (over z, x, y), head: 2 (over core).
Axes of the slice: x: 4, y: 4, z: 4, core: 2. Of those that a mesh axis runs over, the one named last changes fastest.
Arguments:
- queries: bfloat16 [8, 256, 128], P('head', 'kv'), may hold values from -384 to 384
- key_cache: bfloat16 [4096, 8, 128, 128], P('kv', 'head'), may hold values from -6 to 6
- value_cache: bfloat16 [4096, 8, 128, 128], P('kv', 'head'), may hold values from -6 to 6
- key_new: bfloat16 [32, 8, 128], P(None, 'head'), may hold values from -6 to 6
- value_new: bfloat16 [32, 8, 128], P(None, 'head'), may hold values from -6 to 6
- lengths: int32 [32], replicated, may hold values from 2 to 16385, as said below
- page_table: int32 [4096], replicated, may hold values from 0 to 4095, each once
Outputs:
- attended: bfloat16 [8, 256, 128], P('head', 'kv')
Inputs may be any that keep to these rules, and one draw needn't show every extreme that they name: The cache holds the first lengths[s] - 1 tokens of sequence s; some sequence has the largest length. `page_table`: every page appears once; page g lies on kv index g // 64.
All inputs are finite; a program needn't handle non-finite values.
Results may differ from a plain program's by a relative error of at most 0.0025.
Values may be sent and summed in bfloat16 or wider, within the bound.
A program may use at most 64 MiB of HBM per device.

v0:
```python
import math

import jax
import jax.numpy as jnp
from jax import lax
from jax.sharding import PartitionSpec as P

LOWEST_SCORE = -1e30


def in_order(pieces, dim):
    pieces = jnp.moveaxis(pieces, 0, dim)
    shape = pieces.shape
    return pieces.reshape(*shape[:dim], shape[dim] * shape[dim + 1], *shape[dim + 2 :])


def from_everyone(x, axis):
    length = lax.axis_size(axis)
    return lax.all_to_all(jnp.broadcast_to(x[None], (length, *x.shape)), axis, 0, 0, tiled=True)


def collect(x, axis, dim):
    return in_order(from_everyone(x, axis), dim)


def taken_together(x, axis):
    return from_everyone(x, axis).max(axis=0)


def split_up(x, dim, length):
    shape = x.shape
    pieces = x.reshape(*shape[:dim], length, shape[dim] // length, *shape[dim + 1 :])
    return jnp.moveaxis(pieces, dim, 0)


def summed_on_arrival(x, axis, dim):
    pieces = split_up(x, dim, lax.axis_size(axis))
    arrived = lax.all_to_all(pieces, axis, split_axis=0, concat_axis=0, tiled=True)
    return arrived.sum(axis=0)


def sent_together(arrays, axis, dim, along):
    widths = [math.prod(a.shape[along:]) for a in arrays]
    both = jnp.concatenate(
        [a.reshape(*a.shape[:along], w) for a, w in zip(arrays, widths)], axis=along
    )
    result = summed_on_arrival(both, axis, dim)
    pieces = jnp.split(result, [sum(widths[:k]) for k in range(1, len(widths))], axis=along)
    return tuple(
        (b.reshape(*result.shape[:along], *a.shape[along:]) for a, b in zip(arrays, pieces))
    )


def finish(cache_max, cache_sum, cache_out, query_wide, fresh_key, fresh_value, score_scale):
    new_score = jnp.sum(query_wide * fresh_key.astype(jnp.float32), axis=-1) * score_scale
    highest = jnp.maximum(cache_max, new_score)
    old_part = jnp.exp(cache_max - highest)
    new_part = jnp.exp(new_score - highest)
    numerator = cache_out * old_part[..., None] + new_part[..., None] * fresh_value.astype(
        jnp.float32
    )
    denominator = cache_sum * old_part + new_part
    return (numerator / denominator[..., None]).astype(jnp.bfloat16)


def on_device(queries, key_cache, value_cache, key_new, value_new, lengths, page_table):
    all_query = collect(queries, "kv", 1)
    seq_count = lengths.shape[0]
    page_total = page_table.shape[0]
    pages_here = key_cache.shape[0]
    kv_here = key_cache.shape[1]
    page_len = key_cache.shape[2]
    head_width = key_cache.shape[3]
    rows_all = all_query.shape[1]
    group_size = rows_all // seq_count
    page_slots = page_total // seq_count
    local_rows = queries.shape[1]
    score_scale = 1.0 / math.sqrt(head_width)
    kv_index = lax.axis_index("kv")
    inverse = (
        jnp.zeros((page_total,), jnp.int32)
        .at[page_table]
        .set(jnp.arange(page_total, dtype=jnp.int32))
    )
    local_ids = lax.dynamic_slice_in_dim(inverse, kv_index * pages_here, pages_here)
    page_seq = local_ids // page_slots
    page_slot = local_ids % page_slots
    grouped = all_query.reshape(kv_here, seq_count, group_size, head_width)
    page_query = grouped[:, page_seq]
    scores = (
        jnp.einsum("gpqd,pgtd->pgqt", page_query, key_cache, preferred_element_type=jnp.float32)
        * score_scale
    )
    positions = page_slot[:, None] * page_len + jnp.arange(page_len, dtype=jnp.int32)[None, :]
    in_cache = (positions < (lengths[page_seq] - 1)[:, None])[:, None, None, :]
    masked = jnp.where(in_cache, scores, LOWEST_SCORE)
    page_max = jnp.max(masked, axis=3)
    weights = jnp.where(in_cache, jnp.exp(masked - page_max[..., None]), 0.0)
    page_sum = jnp.sum(weights, axis=3)
    page_out = jnp.einsum(
        "pgqt,pgtd->pgqd",
        weights.astype(jnp.bfloat16),
        value_cache,
        preferred_element_type=jnp.float32,
    )
    member = page_seq[None, :] == jnp.arange(seq_count, dtype=jnp.int32)[:, None]
    seq_best = jnp.max(jnp.where(member[:, :, None, None], page_max[None], LOWEST_SCORE), axis=1)
    factor = jnp.exp(page_max - seq_best[page_seq])
    onehot = member.astype(jnp.float32)
    seq_sum = jnp.einsum("sp,pgq->gsq", onehot, page_sum * factor, precision=lax.Precision.HIGHEST)
    seq_out = jnp.einsum(
        "sp,pgqd->gsqd", onehot, page_out * factor[..., None], precision=lax.Precision.HIGHEST
    )
    seq_max = jnp.transpose(seq_best, (1, 0, 2)).reshape(kv_here, rows_all)
    seq_sum = seq_sum.reshape(kv_here, rows_all)
    seq_out = seq_out.reshape(kv_here, rows_all, head_width)
    global_max = taken_together(seq_max, "kv")
    rescale = jnp.exp(seq_max - global_max)
    cache_out, cache_sum = sent_together(
        (seq_out * rescale[..., None], seq_sum * rescale), "kv", 1, 2
    )
    cache_max = lax.dynamic_slice_in_dim(global_max, kv_index * local_rows, local_rows, 1)
    row_seq = (kv_index * local_rows + jnp.arange(local_rows, dtype=jnp.int32)) // group_size
    fresh_key = jnp.transpose(key_new[row_seq], (1, 0, 2))
    fresh_value = jnp.transpose(value_new[row_seq], (1, 0, 2))
    query_wide = queries.astype(jnp.float32)
    return finish(cache_max, cache_sum, cache_out, query_wide, fresh_key, fresh_value, score_scale)


def solution(mesh):
    placed = (
        P("head", "kv", None),
        P("kv", "head", None, None),
        P("kv", "head", None, None),
        P(None, "head", None),
        P(None, "head", None),
        P(),
        P(),
    )
    return jax.shard_map(
        on_device, mesh=mesh, in_specs=placed, out_specs=P("head", "kv", None), check_vma=False
    )
```

profile of v0, /device:TPU:0, one launch (start us, length us, event | category | flops | bytes accessed | tf_op | source)
XLA Modules:
  0.0 90.9 jit_solution(1076743474031147585)
XLA Ops:
  0.0 1.5 %broadcast_in_dim.78 = bf16[64,4,4,128]{3,2,1,0:T(4,128)(2,1)} broadcast(bf16[4,4,128]{2,1,0:T(4,128)(2,1)} %param.7), dimensions={1,2,3} | broadcast | bytes 266240 | tf_op jit(solution)/shard_map/broadcast_in_dim | solution.py:19
  1.5 11.5 %all-to-all-start = ((bf16[64,4,4,128]{3,2,1,0:T(4,128)(2,1)}), bf16[64,4,4,128]{3,2,1,0:T(4,128)(2,1)S(1)}, u32[]{:S(2)}, u32[]{:S(2)}) async-start(bf16[64,4,4,128]{3,2,1,0:T(4,128)(2,1)} %broadcast_in_dim.78), calls=%async_computation | async-start | bytes 524288 | tf_op jit(solution)/shard_map/all_to_all | solution.py:19
  13.0 0.7 compare_select_fusion
  13.7 15.5 %scatter_custom_fusion = s32[4096]{0:T(1024)S(1)} fusion(s32[4096]{0:T(1024)S(1)} %compare_select_fusion, s32[4096]{0:T(1024)S(1)} %iota.23, s32[]{:T(128)} %constant.32.clone.1), kind=kCustom, calls=%fused_computation.40 | custom fusion | bytes 16388 | tf_op jit(solution)/shard_map/scatter | solution.py:83
  29.3 0.1 fusion.22
  29.3 0.1 compare_select_fusion.2
  29.4 1.4 %gather_fusion = s32[64]{0:T(128)S(1)} fusion(s32[32]{0:T(128)} %param.12, s32[1024]{0:T(1024)S(1)} %pad_clamp_fusion.1), kind=kCustom, calls=%fused_computation | custom fusion | bytes 768 | tf_op jit(solution)/shard_map/gather | solution.py:95
  30.9 0.1 add_compare_fusion
  31.0 0.1 copy.90
  31.1 0.8 gather_fusion.1
  31.9 6.9 %fusion.28 = (f32[64,4,8]{2,1,0:T(4,128)S(1)}, f32[64,4,8,128]{3,2,1,0:T(8,128)S(1)}) fusion(bf16[64,4,128,128]{3,2,1,0:T(8,128)(2,1)} %param.8, bf16[64,4,8,128]{3,2,1,0:T(8,128)(2,1)S(1)} %gather_fusion.1, pred[64,128]{1,0:T(8,128)(4,1)S(1)} %add_compare_fusion), kind=kOutput, calls=%fused_computation.66 | convolution fusion | flops 67893248 | bytes 9977856 | tf_op jit(solution)/shard_map/gpqd,pgtd->pgqt/dot_general | solution.py:91
  38.9 0.3 select_reduce_fusion
  39.2 0.7 gather_fusion.2
  39.9 0.8 fusion.2
  40.6 0.1 broadcast_in_dim.84
  40.7 0.7 broadcast_in_dim.85
  41.5 10.3 %all-to-all-start.1 = ((f32[64,4,256]{2,1,0:T(4,128)}), f32[64,4,256]{2,1,0:T(4,128)S(1)}, u32[]{:S(2)}, u32[]{:S(2)}) async-start(f32[64,4,256]{2,1,0:T(4,128)} %broadcast_in_dim.85), calls=%async_computation.1 | async-start | bytes 524288 | tf_op jit(solution)/shard_map/all_to_all | solution.py:19
  51.8 4.7 %convolution_multiply_fusion = f32[64,4,8,128]{3,2,1,0:T(8,128)S(1)} fusion(bf16[64,4,128,128]{3,2,1,0:T(8,128)(2,1)} %param.9, f32[64,4,8,128]{3,2,1,0:T(8,128)S(1)} %get-tuple-element.15, f32[64,4,8]{2,1,0:T(4,128)S(1)} %bitcast.50, f32[64,4,8]{2,1,0:T(4,128)S(1)} %get-tuple-element.14, pred[64,128]{1,0:T(8,128)(4,1)S(1)} %add_compare_fusion), kind=kOutput, calls=%fused_computation.6 | convolution fusion | flops 68157440 | bytes 10510336 | tf_op jit(solution)/shard_map/pgqt,pgtd->pgqd/dot_general | solution.py:100
  56.6 1.1 %convolution_bitcast_fusion = f32[4,32,8,128]{3,1,2,0:T(8,128)S(1)} fusion(f32[64,4,8,128]{3,2,1,0:T(8,128)S(1)} %convolution_multiply_fusion, s32[64]{0:T(128)S(1)} %get-tuple-element.13), kind=kOutput, calls=%fused_computation.9 | convolution fusion | flops 100665344 | bytes 1573120 | tf_op jit(solution)/shard_map/sp,pgqd->gsqd/dot_general | solution.py:111
  57.7 0.1 reshape.189
  57.8 0.1 reshape.191
  57.9 0.3 copy.93
  58.2 0.3 convolution_bitcast_fusion.1
  58.5 0.1 reshape.190
  58.6 0.1 copy.102
  58.7 0.1 copy.100
  58.8 3.5 %all-to-all-done.1 = f32[64,4,256]{2,1,0:T(4,128)S(1)} async-done(((f32[64,4,256]{2,1,0:T(4,128)}), f32[64,4,256]{2,1,0:T(4,128)S(1)}, u32[]{:S(2)}, u32[]{:S(2)}) %all-to-all-start.1) | async-done | bytes 262176 | tf_op jit(solution)/shard_map/all_to_all | solution.py:19
  62.4 0.1 reduce_max.33
  62.5 0.1 reduce_max.34
  62.6 0.1 reduce_max.35
  62.8 0.1 copy.101
  62.9 0.3 copy.103
  63.2 0.3 broadcast_multiply_fusion
  63.6 0.3 maximum_bitcast_fusion
  63.8 1.3 %copy.104 = f32[64,4,4,129]{3,2,1,0:T(4,128)} copy(f32[64,4,4,129]{3,2,0,1:T(4,128)S(1)} %maximum_bitcast_fusion) | data formatting | bytes 1056768 | tf_op jit(solution)/shard_map/transpose | solution.py:33
  65.1 6.8 %all-to-all-start.2 = ((f32[64,4,4,129]{3,2,1,0:T(4,128)}), f32[64,4,4,129]{3,2,1,0:T(4,128)S(1)}, u32[]{:S(2)}, u32[]{:S(2)}) async-start(f32[64,4,4,129]{3,2,1,0:T(4,128)} %copy.104), calls=%async_computation.2 | async-start | bytes 2097152 | tf_op jit(solution)/shard_map/all_to_all | solution.py:38
  72.0 0.6 gather_fusion.3
  72.6 0.1 fusion.14
  72.7 0.1 copy.108
  72.8 1.3 %gather_fusion.4 = bf16[4,4,128]{2,1,0:T(4,128)(2,1)S(1)} fusion(bf16[32,4,128]{2,1,0:T(4,128)(2,1)} %param.11, s32[1024]{0:T(1024)S(1)} %pad_clamp_fusion), kind=kCustom, calls=%fused_computation.4 | custom fusion | bytes 8208 | tf_op jit(solution)/shard_map/gather | solution.py:125
  74.1 15.5 %all-to-all-done.2 = f32[64,4,4,129]{3,2,1,0:T(4,128)S(1)} async-done(((f32[64,4,4,129]{3,2,1,0:T(4,128)}), f32[64,4,4,129]{3,2,1,0:T(4,128)S(1)}, u32[]{:S(2)}, u32[]{:S(2)}) %all-to-all-start.2) | async-done | bytes 528416 | tf_op jit(solution)/shard_map/all_to_all | solution.py:38
  89.6 0.2 reduce_sum.28
  89.8 0.1 slice_reduce_fusion
  89.9 0.1 copy.109
  90.0 0.1 copy.110
  90.1 0.1 copy.111
  90.2 0.1 fusion.19
  90.3 0.6 copy.112
  (19 shorter events, 0.4 us)
Async XLA Ops:
  0.0 72.0 %copy-start = (bf16[32,4,128]{2,1,0:T(4,128)(2,1)S(1)}, bf16[32,4,128]{2,1,0:T(4,128)(2,1)}, u32[]{:S(2)}) copy-start(bf16[32,4,128]{2,1,0:T(4,128)(2,1)} %param.10) | copy-start | bytes 98308
  1.5 29.5 %all-to-all-start = ((bf16[64,4,4,128]{3,2,1,0:T(4,128)(2,1)}), bf16[64,4,4,128]{3,2,1,0:T(4,128)(2,1)S(1)}, u32[]{:S(2)}, u32[]{:S(2)}) async-start(bf16[64,4,4,128]{3,2,1,0:T(4,128)(2,1)} %broadcast_in_dim.78), calls=%async_computation | async-start | bytes 524288 | tf_op jit(solution)/shard_map/all_to_all | solution.py:19
  41.5 20.9 %all-to-all-start.1 = ((f32[64,4,256]{2,1,0:T(4,128)}), f32[64,4,256]{2,1,0:T(4,128)S(1)}, u32[]{:S(2)}, u32[]{:S(2)}) async-start(f32[64,4,256]{2,1,0:T(4,128)} %broadcast_in_dim.85), calls=%async_computation.1 | async-start | bytes 524288 | tf_op jit(solution)/shard_map/all_to_all | solution.py:19
  56.6 16.0 %copy-start.1 = (bf16[4,4,128]{2,1,0:T(4,128)(2,1)S(1)}, bf16[4,4,128]{2,1,0:T(4,128)(2,1)}, u32[]{:S(2)}) copy-start(bf16[4,4,128]{2,1,0:T(4,128)(2,1)} %param.7) | copy-start | bytes 12292
  65.1 24.4 %all-to-all-start.2 = ((f32[64,4,4,129]{3,2,1,0:T(4,128)}), f32[64,4,4,129]{3,2,1,0:T(4,128)S(1)}, u32[]{:S(2)}, u32[]{:S(2)}) async-start(f32[64,4,4,129]{3,2,1,0:T(4,128)} %copy.104), calls=%async_computation.2 | async-start | bytes 2097152 | tf_op jit(solution)/shard_map/all_to_all | solution.py:38
where the time goes:
time: 91.4 us; the launch traced here: 90.9 us
  starting transfers between devices  28.7 us (31%)
  local copies, waits for them, and re-layouts  26.6 us (29%)
  waiting for transfers between devices  19 us (21%)
  matrix products  13 us (14%)
  other arithmetic  3.3 us (4%)
    all_to_all x2, starting transfers between devices, from_everyone(): lax.all_to_all(jnp.broadcast_to(x[None], (length, *x.shape)), axis, 0, 0,...  21.9 us
    scatter x1, local copies, waits for them, and re-layouts, on_device(): inverse = jnp.zeros((page_total,), jnp.int32).at[page_table].set(jnp.aran...  15.5 us
    all_to_all x1, waiting for transfers between devices, summed_on_arrival(): lax.all_to_all(pieces, axis, split_axis=0, concat_axis=0, tiled=True)  15.5 us
    dot_general x1, matrix products, on_device(): jnp.einsum('gpqd,pgtd->pgqt', page_query, key_cache, preferred_element_ty...  6.95 us
    all_to_all x1, starting transfers between devices, summed_on_arrival(): lax.all_to_all(pieces, axis, split_axis=0, concat_axis=0, tiled=True)  6.82 us
    dot_general x1, matrix products, on_device(): jnp.einsum('pgqt,pgtd->pgqd', weights.astype(jnp.bfloat16), value_cache,...  4.74 us
    all_to_all x2, waiting for transfers between devices, from_everyone(): lax.all_to_all(jnp.broadcast_to(x[None], (length, *x.shape)), axis, 0, 0,...  3.53 us
    broadcast_in_dim x3, local copies, waits for them, and re-layouts, from_everyone(): jnp.broadcast_to(x[None], (length, *x.shape))  2.28 us
  transfers between devices with their start and end apart: 3, of which 2 were waited for; matrix products, arithmetic and copies ran while one was open for 30% of the time, Pallas kernels for 0%

commit v1 on v0

v1 whole, which is shorter than its diff:
```python
import functools
import math

import jax
import jax.numpy as jnp
from jax import lax
from jax.experimental import pallas as pl
from jax.experimental.pallas import tpu as pltpu
from jax.sharding import PartitionSpec as P

LOW = -1e30
FLOOR = -5e29
F32 = jnp.float32
BF16 = jnp.bfloat16


def hops(t):
    total = 0
    while t:
        total += (0, 1, 2, 1)[t % 4]
        t //= 4
    return total


def iota(shape, dim):
    return lax.broadcasted_iota(jnp.int32, shape, dim)


def dot(a, b, dims=((1,), (0,))):
    return lax.dot_general(a, b, (dims, ((), ())), preferred_element_type=F32)


def kernel(
    n, q_ref, k_hbm, v_hbm, kn_ref, vn_ref, len_ref, tbl_ref, out_ref,
    kbuf, vbuf, qall, racc, rml, sbuf, sacc, sstat, gacc, gstat, meta_v, meta_s,
    ksem, vsem, msem, qs_sem, qr_sem, as_sem, ar_sem, ss_sem, sr_sem,
):
    pages, heads, page_len, width = kbuf.shape
    seqs = len_ref.shape[0]
    slots = tbl_ref.shape[1]
    me = lax.axis_index("kv")
    head = lax.axis_index("head")
    c = math.log2(math.e) / math.sqrt(width)
    order = sorted(range(1, n), key=hops, reverse=True)

    def peer(t):
        return (jnp.bitwise_xor(me, t), head)

    parts = 8
    step = pages // parts
    for hbm, buf, sem in ((k_hbm, kbuf, ksem), (v_hbm, vbuf, vsem)):
        for i in range(parts):
            pltpu.make_async_copy(hbm.at[pl.ds(i * step, step)], buf.at[pl.ds(i * step, step)], sem).start()

    barrier = pltpu.get_barrier_semaphore()
    for t in order:
        pl.semaphore_signal(barrier, inc=1, device_id=peer(t), device_id_type=pl.DeviceIdType.MESH)

    q16 = q_ref[...].astype(F32).reshape(16, width)
    qall[me] = q16.astype(BF16)

    pl.semaphore_wait(barrier, n - 1)
    for t in order:
        pltpu.make_async_remote_copy(
            src_ref=qall.at[me], dst_ref=qall.at[me], send_sem=qs_sem, recv_sem=qr_sem,
            device_id=peer(t), device_id_type=pl.DeviceIdType.MESH,
        ).start()

    rel = tbl_ref[...] - me * pages
    here = jnp.logical_and(rel >= 0, rel < pages)
    here_f = jnp.where(here, 1.0, 0.0)
    here_b = here_f.astype(BF16)
    upper = jnp.where(iota((slots, slots), 0) < iota((slots, slots), 1), 1.0, 0.0).astype(BF16)
    ones = jnp.full((slots, slots), 1.0, BF16)
    lower = jnp.where(iota((seqs, seqs), 1) < iota((seqs, seqs), 0), 1.0, 0.0).astype(BF16)
    in_row = dot(here_b, upper)
    row_total = dot(here_b, ones)
    before = dot(lower, row_total.astype(BF16))
    place = jnp.where(here, in_row + before, -1.0)
    value = ((iota((seqs, slots), 0) * slots + iota((seqs, slots), 1)) * pages + rel).astype(F32)
    value = jnp.where(here, value, 0.0)
    kth = iota((pages, slots), 0).astype(F32)
    found = jnp.zeros((pages, slots), F32)
    for s in range(seqs):
        found = found + jnp.where(place[s : s + 1] == kth, value[s : s + 1], 0.0)
    found = jnp.sum(found, axis=1, keepdims=True)
    lane = iota((pages, slots), 1)
    row = jnp.sum(jnp.where(lane == iota((pages, slots), 0), found, 0.0), axis=0, keepdims=True)
    ends = before + row_total
    lane = iota((seqs, slots), 1)
    row = row + jnp.sum(jnp.where(lane == iota((seqs, slots), 0) + pages, ends, 0.0), axis=0, keepdims=True)
    meta_v[...] = row.astype(jnp.int32)
    copy = pltpu.make_async_copy(meta_v, meta_s, msem)
    copy.start()

    owned = me // 2
    row_g = iota((16, width), 0) // 4
    kn = kn_ref[owned].astype(F32)
    vn = vn_ref[owned].astype(F32)
    kn16 = jnp.zeros((16, width), F32)
    vn16 = jnp.zeros((16, width), F32)
    for g in range(heads):
        kn16 = jnp.where(row_g == g, kn[g : g + 1], kn16)
        vn16 = jnp.where(row_g == g, vn[g : g + 1], vn16)
    new_raw = jnp.sum(q16 * kn16, axis=1, keepdims=True)

    copy.wait()
    pltpu.make_async_copy(k_hbm, kbuf, ksem).wait()
    pltpu.make_async_copy(v_hbm, vbuf, vsem).wait()
    pltpu.make_async_copy(qall.at[pl.ds(0, n - 1)], qall.at[pl.ds(0, n - 1)], qr_sem).wait()

    low_half = iota((8, page_len), 0) < 4
    low_half16 = iota((16, page_len), 0) % 8 < 4
    lanes = iota((32, page_len), 1)
    chunk = sbuf.shape[0]
    page_bits = pages.bit_length() - 1
    slot_bits = slots.bit_length() - 1

    def decode(k):
        code = meta_s[0, k]
        slot = jnp.bitwise_and(code >> page_bits, slots - 1)
        seq = jnp.bitwise_and(code >> (page_bits + slot_bits), seqs - 1)
        return jnp.bitwise_and(code, pages - 1), seq, slot

    def scores(k):
        p, s, _ = decode(k)
        qb = qall[pl.ds(2 * s, 2)].reshape(32, width)
        raw = dot(qb, kbuf[p].reshape(heads * page_len, width), ((1,), (1,)))
        tiles = []
        for rb in range(4):
            g = 2 * (rb % 2)
            mine = raw[rb * 8 : rb * 8 + 8]
            tiles.append(jnp.where(low_half, mine[:, g * 128 : g * 128 + 128], mine[:, g * 128 + 128 : g * 128 + 256]))
        return jnp.concatenate(tiles, axis=0)

    def attend(k, raw, state):
        m, l, acc = state
        p, s, slot = decode(k)
        before_seq = decode(jnp.maximum(k - 1, 0))[1]
        first = jnp.logical_or(k == 0, before_seq != s)
        valid = len_ref[s] - 1 - slot * page_len
        raw = jnp.where(lanes < valid, raw, LOW)
        top = jnp.maximum(jnp.max(raw, axis=1, keepdims=True), FLOOR)
        weights = jnp.exp2((raw - top) * c)
        total = jnp.sum(weights, axis=1, keepdims=True)
        outs = []
        for pair in range(2):
            both = jnp.concatenate(
                [weights[pair * 8 : pair * 8 + 8], weights[16 + pair * 8 : 16 + pair * 8 + 8]], axis=0
            )
            lhs = jnp.concatenate(
                [jnp.where(low_half16, both, 0.0).astype(BF16), jnp.where(low_half16, 0.0, both).astype(BF16)], axis=1
            )
            rhs = vbuf[p, pl.ds(2 * pair, 2)].reshape(2 * page_len, width)
            outs.append(dot(lhs, rhs))
        page_out = jnp.concatenate([outs[0][:8], outs[1][:8], outs[0][8:], outs[1][8:]], axis=0)
        top = jnp.broadcast_to(top, m.shape)
        m = jnp.where(first, FLOOR, m)
        new_m = jnp.maximum(m, top)
        old = jnp.where(first, 0.0, jnp.exp2((m - new_m) * c))
        new = jnp.exp2((top - new_m) * c)
        l = l * old + total * new
        acc = acc * old + page_out * new
        racc[k] = acc
        rml[k] = jnp.where(lanes < 64, new_m, l)
        return new_m, l, acc

    for i in range(chunk):
        sbuf[i] = scores(i)

    def body(i, state):
        raws = [sbuf[u] for u in range(chunk)]
        for u in range(chunk):
            sbuf[u] = scores((i + 1) * chunk + u)
        for u in range(chunk):
            state = attend(i * chunk + u, raws[u], state)
        return state

    zero = jnp.zeros((32, width), F32)
    steps = pages // chunk
    state = lax.fori_loop(0, steps - 1, body, (zero, zero, zero))
    for u in range(chunk):
        state = attend((steps - 1) * chunk + u, sbuf[u], state)

    lane16 = iota((16, width), 1) % 64

    def gather(s, stat):
        end = meta_s[0, pages + s]
        start = jnp.where(s == 0, 0, meta_s[0, pages + jnp.maximum(s - 1, 0)])
        some = end > start
        last = jnp.clip(end - 1, 0, pages - 1)
        acc = jnp.where(some, racc[last], 0.0)
        ml = jnp.where(some, rml[last], jnp.where(lanes < 64, FLOOR, 0.0))
        sacc[2 * s] = acc[:16]
        sacc[2 * s + 1] = acc[16:]
        stat = jnp.where(lane16 == 2 * s, ml[:16], stat)
        return jnp.where(lane16 == 2 * s + 1, ml[16:], stat)

    stat = lax.fori_loop(0, seqs, gather, jnp.zeros((16, width), F32), unroll=4)
    for t in order:
        to = jnp.bitwise_xor(me, t)
        pltpu.make_async_remote_copy(
            src_ref=sacc.at[to], dst_ref=gacc.at[me], send_sem=as_sem, recv_sem=ar_sem,
            device_id=peer(t), device_id_type=pl.DeviceIdType.MESH,
        ).start()
    turned = jnp.concatenate([stat] * 8, axis=0).T
    sstat[:, 0, :] = turned[:n]
    sstat[:, 1, :] = turned[n:]
    for t in order:
        to = jnp.bitwise_xor(me, t)
        pltpu.make_async_remote_copy(
            src_ref=sstat.at[to], dst_ref=gstat.at[me], send_sem=ss_sem, recv_sem=sr_sem,
            device_id=peer(t), device_id_type=pl.DeviceIdType.MESH,
        ).start()
    gacc[me] = sacc[me]
    gstat[me] = sstat[me]

    some_q, some_a, some_s = (r.at[pl.ds(0, n - 1)] for r in (qall, gacc, gstat))
    pltpu.make_async_copy(some_s, some_s, sr_sem).wait()
    tops = gstat[:, 0, :]
    sums = gstat[:, 1, :]
    top = jnp.max(tops, axis=0, keepdims=True)
    w = jnp.exp2((tops - top) * c)
    total = jnp.sum(w * sums, axis=0, keepdims=True)
    at_row = iota((16, width), 1) % 16 == iota((16, width), 0)
    first16 = jnp.logical_and(at_row, iota((16, width), 1) < 16)
    top16 = jnp.sum(jnp.where(first16, top, 0.0), axis=1, keepdims=True)
    sum16 = jnp.sum(jnp.where(first16, total, 0.0), axis=1, keepdims=True)
    mine = iota((8, width), 1) // 16 == iota((8, width), 0)
    blocks = []
    for b in range(n // 8):
        line = jnp.sum(jnp.where(mine, w[8 * b : 8 * b + 8], 0.0), axis=0, keepdims=True)
        blocks.append(jnp.where(at_row, line, 0.0))
    wide = jnp.concatenate(blocks, axis=1)
    wide_hi = wide.astype(BF16)
    wide_lo = (wide - wide_hi.astype(F32)).astype(BF16)
    high = jnp.maximum(top16, new_raw)
    old = jnp.exp2((top16 - high) * c)
    new = jnp.exp2((new_raw - high) * c)
    pltpu.make_async_copy(some_a, some_a, ar_sem).wait()
    sent = gacc[...].reshape(16 * n, width)
    sent_hi = sent.astype(BF16)
    sent_lo = (sent - sent_hi.astype(F32)).astype(BF16)
    both = dot(jnp.concatenate([wide_hi, wide_lo], axis=0), sent_hi)
    numer = (both[:16] + both[16:] + dot(wide_hi, sent_lo)) * old + new * vn16
    out_ref[...] = (numer / (sum16 * old + new)).astype(BF16)

    pltpu.make_async_copy(some_q, some_q, qs_sem).wait()
    pltpu.make_async_copy(some_a, some_a, as_sem).wait()
    pltpu.make_async_copy(some_s, some_s, ss_sem).wait()


def on_device(queries, key_cache, value_cache, key_new, value_new, lengths, page_table):
    n = lax.axis_size("kv")
    heads, rows, width = queries.shape
    pages, _, page_len, _ = key_cache.shape
    seqs = lengths.shape[0]
    vmem = pl.BlockSpec(memory_space=pltpu.VMEM)
    hbm = pl.BlockSpec(memory_space=pltpu.HBM)
    dma = pltpu.SemaphoreType.DMA
    out = pl.pallas_call(
        functools.partial(kernel, n),
        out_shape=jax.ShapeDtypeStruct((heads * rows, width), BF16),
        in_specs=[vmem, hbm, hbm, vmem, vmem, pl.BlockSpec(memory_space=pltpu.SMEM), vmem],
        out_specs=vmem,
        scratch_shapes=[
            pltpu.VMEM(key_cache.shape, BF16),
            pltpu.VMEM(value_cache.shape, BF16),
            pltpu.VMEM((n, 16, width), BF16),
            pltpu.VMEM((pages, 32, width), F32),
            pltpu.VMEM((pages, 32, width), F32),
            pltpu.VMEM((4, 32, page_len), F32),
            pltpu.VMEM((n, 16, width), F32),
            pltpu.VMEM((n, 2, width), F32),
            pltpu.VMEM((n, 16, width), F32),
            pltpu.VMEM((n, 2, width), F32),
            pltpu.VMEM((1, width), jnp.int32),
            pltpu.SMEM((1, width), jnp.int32),
            *[dma] * 9,
        ],
        compiler_params=pltpu.CompilerParams(
            collective_id=0, has_side_effects=True
        ),
    )(queries, key_cache, value_cache, key_new, value_new, lengths, page_table.reshape(seqs, -1))
    return out.reshape(heads, rows, width)


def solution(mesh):
    placed = (
        P("head", "kv", None),
        P("kv", "head", None, None),
        P("kv", "head", None, None),
        P(None, "head", None),
        P(None, "head", None),
        P(),
        P(),
    )
    return jax.shard_map(
        on_device, mesh=mesh, in_specs=placed, out_specs=P("head", "kv", None), check_vma=False
    )
```

time: 91.4 us -> 35 us (0.38)
  Pallas kernels: 0 us -> 33.5 us
  starting transfers between devices: 28.7 us -> 0 us
  local copies, waits for them, and re-layouts: 26.6 us -> 1.28 us
  waiting for transfers between devices: 19 us -> 0 us
  matrix products: 13 us -> 0 us
  other arithmetic: 3.3 us -> 0 us
    pallas_call x0 -> x1, Pallas kernels: none -> 33.5 us  [on_device(): pl.pallas_call(functools.partial(kernel, n), out_shape=jax.ShapeDtypeStru...]
    all_to_all x3 -> x0, starting transfers between devices: 28.7 us -> none  [the longest x2 21.9 us: from_everyone(): lax.all_to_all(jnp.broadcast_to(x[None], (length, *x.shape)), axis, 0, 0,...]
    all_to_all x3 -> x0, waiting for transfers between devices: 19 us -> none  [the longest x1 15.5 us: summed_on_arrival(): lax.all_to_all(pieces, axis, split_axis=0, concat_axis=0, tiled=True)]
    scatter x1 -> x0, local copies, waits for them, and re-layouts: 15.5 us -> none  [on_device(): inverse = jnp.zeros((page_total,), jnp.int32).at[page_table].set(jnp.aran...]
    dot_general x4 -> x0, matrix products: 13 us -> none  [the longest x1 6.95 us: on_device(): jnp.einsum('gpqd,pgtd->pgqt', page_query, key_cache, preferred_element_ty...]
    gather x5 -> x0, local copies, waits for them, and re-layouts: 4.78 us -> none  [the longest x1 1.43 us: on_device(): in_cache = (positions < (lengths[page_seq] - 1)[:, None])[:, None, None, :]]
    broadcast_in_dim x3 -> x0, local copies, waits for them, and re-layouts: 2.28 us -> none  [from_everyone(): jnp.broadcast_to(x[None], (length, *x.shape))]
    transpose x5 -> x0, local copies, waits for them, and re-layouts: 1.8 us -> none  [the longest x1 1.31 us: split_up(): return jnp.moveaxis(pieces, dim, 0)]
  transfers between devices with their start and end apart: 3 -> 0, of which waited for: 2 -> 0; matrix products, arithmetic and copies ran while one was open for 30% -> 0% of each run, Pallas kernels for 0% -> 0%
where the time goes in v1:
time: 35 us; the launch traced here: 34.8 us
  Pallas kernels  33.5 us (96%)
  local copies, waits for them, and re-layouts  1.28 us (4%)
    pallas_call x1, Pallas kernels, on_device(): pl.pallas_call(functools.partial(kernel, n), out_shape=jax.ShapeDtypeStru...  33.5 us
    unnamed x1, local copies, waits for them, and re-layouts  1.28 us

profile of v1, /device:TPU:0, one launch (start us, length us, event | category | flops | bytes accessed | tf_op | source)
XLA Modules:
  0.0 34.8 jit_solution(11274765533892838201)
XLA Ops:
  0.0 33.5 %shard_map.73 = bf16[16,128]{1,0:T(8,128)(2,1)} custom-call(bf16[4,4,128]{2,1,0:T(4,128)(2,1)} %q_ref.1, bf16[64,4,128,128]{3,2,1,0:T(8,128)(2,1)} %k_hbm.1, bf16[64,4,128,128]{3,2,1,0:T(8,128)(2,1)} %v_hbm.1, bf16[32,4,128]{2,1,0:T(4,128)(2,1)} %kn_ref.1, bf16[32,4,128]{2,1,0:T(4,128)(2,1)} %vn_ref.1, s32[32]{0:T(128)} %len_ref.1, s32[32,128]{1,0:T(8,128)} %bitcast.2), custom_call_target="tpu_custom_call" | custom-call | tf_op jit(solution)/shard_map/pallas_call | solution.py:261
  33.5 1.3 %copy.9 = bf16[4,4,128]{2,1,0:T(4,128)(2,1)} copy(bf16[4,4,128]{2,1,0:T(4,128)(2,1)} %bitcast.3) | data formatting | bytes 8192

commit v2 on v1

--- a/solution.py
+++ b/solution.py
@@ -31,9 +31,10 @@
 
 
 def kernel(
-    n, q_ref, k_hbm, v_hbm, kn_ref, vn_ref, len_ref, tbl_ref, out_ref,
+    n, q_hbm, k_hbm, v_hbm, kn_hbm, vn_hbm, len_hbm, tbl_hbm, out_ref,
+    q_ref, kn_ref, vn_ref, len_ref, tbl_ref,
     kbuf, vbuf, qall, racc, rml, sbuf, sacc, sstat, gacc, gstat, meta_v, meta_s,
-    ksem, vsem, msem, qs_sem, qr_sem, as_sem, ar_sem, ss_sem, sr_sem,
+    ksem, vsem, qsem, insem, lsem, msem, qs_sem, qr_sem, as_sem, ar_sem, ss_sem, sr_sem,
 ):
     pages, heads, page_len, width = kbuf.shape
     seqs = len_ref.shape[0]
@@ -46,25 +47,35 @@
     def peer(t):
         return (jnp.bitwise_xor(me, t), head)
 
+    barrier = pltpu.get_barrier_semaphore()
+    for t in order:
+        pl.semaphore_signal(barrier, inc=1, device_id=peer(t), device_id_type=pl.DeviceIdType.MESH)
+
+    owned = me // 2
+    q_copy = pltpu.make_async_copy(q_hbm, q_ref, qsem)
+    q_copy.start()
+    len_copy = pltpu.make_async_copy(len_hbm, len_ref, lsem)
+    len_copy.start()
+    small = [
+        pltpu.make_async_copy(tbl_hbm, tbl_ref, insem.at[0]),
+        pltpu.make_async_copy(kn_hbm.at[owned], kn_ref, insem.at[1]),
+        pltpu.make_async_copy(vn_hbm.at[owned], vn_ref, insem.at[2]),
+    ]
+    for one in small:
+        one.start()
+    q_copy.wait()
+    len_copy.wait()
+    for one in small:
+        one.wait()
     parts = 8
     step = pages // parts
     for hbm, buf, sem in ((k_hbm, kbuf, ksem), (v_hbm, vbuf, vsem)):
         for i in range(parts):
             pltpu.make_async_copy(hbm.at[pl.ds(i * step, step)], buf.at[pl.ds(i * step, step)], sem).start()
 
-    barrier = pltpu.get_barrier_semaphore()
-    for t in order:
-        pl.semaphore_signal(barrier, inc=1, device_id=peer(t), device_id_type=pl.DeviceIdType.MESH)
-
     q16 = q_ref[...].astype(F32).reshape(16, width)
     qall[me] = q16.astype(BF16)
 
-    pl.semaphore_wait(barrier, n - 1)
-    for t in order:
-        pltpu.make_async_remote_copy(
-            src_ref=qall.at[me], dst_ref=qall.at[me], send_sem=qs_sem, recv_sem=qr_sem,
-            device_id=peer(t), device_id_type=pl.DeviceIdType.MESH,
-        ).start()
 
     rel = tbl_ref[...] - me * pages
     here = jnp.logical_and(rel >= 0, rel < pages)
@@ -93,10 +104,9 @@
     copy = pltpu.make_async_copy(meta_v, meta_s, msem)
     copy.start()
 
-    owned = me // 2
     row_g = iota((16, width), 0) // 4
-    kn = kn_ref[owned].astype(F32)
-    vn = vn_ref[owned].astype(F32)
+    kn = kn_ref[...].astype(F32)
+    vn = vn_ref[...].astype(F32)
     kn16 = jnp.zeros((16, width), F32)
     vn16 = jnp.zeros((16, width), F32)
     for g in range(heads):
@@ -105,11 +115,19 @@
     new_raw = jnp.sum(q16 * kn16, axis=1, keepdims=True)
 
     copy.wait()
+
+    pl.semaphore_wait(barrier, n - 1)
+    for t in order:
+        pltpu.make_async_remote_copy(
+            src_ref=qall.at[me], dst_ref=qall.at[me], send_sem=qs_sem, recv_sem=qr_sem,
+            device_id=peer(t), device_id_type=pl.DeviceIdType.MESH,
+        ).start()
+
     pltpu.make_async_copy(k_hbm, kbuf, ksem).wait()
     pltpu.make_async_copy(v_hbm, vbuf, vsem).wait()
     pltpu.make_async_copy(qall.at[pl.ds(0, n - 1)], qall.at[pl.ds(0, n - 1)], qr_sem).wait()
 
-    low_half = iota((8, page_len), 0) < 4
+    even = (iota((32, width), 0) // 4) % 2 == 0
     low_half16 = iota((16, page_len), 0) % 8 < 4
     lanes = iota((32, page_len), 1)
     chunk = sbuf.shape[0]
@@ -125,13 +143,16 @@
     def scores(k):
         p, s, _ = decode(k)
         qb = qall[pl.ds(2 * s, 2)].reshape(32, width)
-        raw = dot(qb, kbuf[p].reshape(heads * page_len, width), ((1,), (1,)))
-        tiles = []
-        for rb in range(4):
-            g = 2 * (rb % 2)
-            mine = raw[rb * 8 : rb * 8 + 8]
-            tiles.append(jnp.where(low_half, mine[:, g * 128 : g * 128 + 128], mine[:, g * 128 + 128 : g * 128 + 256]))
-        return jnp.concatenate(tiles, axis=0)
+        none = jnp.zeros_like(qb)
+        lhs = jnp.concatenate([jnp.where(even, qb, none), jnp.where(even, none, qb)], axis=1)
+        keys = kbuf[p]
+        rhs = jnp.concatenate(
+            [jnp.concatenate([keys[0], keys[1]], axis=1), jnp.concatenate([keys[2], keys[3]], axis=1)], axis=0
+        )
+        raw = dot(lhs, rhs, ((1,), (1,)))
+        return jnp.concatenate(
+            [raw[0:8, :page_len], raw[8:16, page_len:], raw[16:24, :page_len], raw[24:32, page_len:]], axis=0
+        )
 
     def attend(k, raw, state):
         m, l, acc = state
@@ -243,7 +264,7 @@
     sent_lo = (sent - sent_hi.astype(F32)).astype(BF16)
     both = dot(jnp.concatenate([wide_hi, wide_lo], axis=0), sent_hi)
     numer = (both[:16] + both[16:] + dot(wide_hi, sent_lo)) * old + new * vn16
-    out_ref[...] = (numer / (sum16 * old + new)).astype(BF16)
+    out_ref[...] = (numer / (sum16 * old + new)).reshape(out_ref.shape).astype(BF16)
 
     pltpu.make_async_copy(some_q, some_q, qs_sem).wait()
     pltpu.make_async_copy(some_a, some_a, as_sem).wait()
@@ -260,29 +281,38 @@
     dma = pltpu.SemaphoreType.DMA
     out = pl.pallas_call(
         functools.partial(kernel, n),
-        out_shape=jax.ShapeDtypeStruct((heads * rows, width), BF16),
-        in_specs=[vmem, hbm, hbm, vmem, vmem, pl.BlockSpec(memory_space=pltpu.SMEM), vmem],
+        out_shape=jax.ShapeDtypeStruct(queries.shape, BF16),
+        in_specs=[hbm] * 7,
         out_specs=vmem,
         scratch_shapes=[
+            pltpu.VMEM(queries.shape, BF16),
+            pltpu.VMEM((heads, width), BF16),
+            pltpu.VMEM((heads, width), BF16),
+            pltpu.SMEM((seqs,), jnp.int32),
+            pltpu.VMEM((seqs, page_table.shape[0] // seqs), jnp.int32),
             pltpu.VMEM(key_cache.shape, BF16),
             pltpu.VMEM(value_cache.shape, BF16),
             pltpu.VMEM((n, 16, width), BF16),
             pltpu.VMEM((pages, 32, width), F32),
             pltpu.VMEM((pages, 32, width), F32),
-            pltpu.VMEM((4, 32, page_len), F32),
+            pltpu.VMEM((16, 32, page_len), F32),
             pltpu.VMEM((n, 16, width), F32),
             pltpu.VMEM((n, 2, width), F32),
             pltpu.VMEM((n, 16, width), F32),
             pltpu.VMEM((n, 2, width), F32),
             pltpu.VMEM((1, width), jnp.int32),
             pltpu.SMEM((1, width), jnp.int32),
-            *[dma] * 9,
+            dma,
+            dma,
+            dma,
+            dma((3,)),
+            *[dma] * 8,
         ],
         compiler_params=pltpu.CompilerParams(
             collective_id=0, has_side_effects=True
         ),
     )(queries, key_cache, value_cache, key_new, value_new, lengths, page_table.reshape(seqs, -1))
-    return out.reshape(heads, rows, width)
+    return out
 
 
 def solution(mesh):

time: 35 us -> 32.5 us (0.929)
  Pallas kernels: 33.5 us -> 31 us
    pallas_call x1, Pallas kernels: 33.5 us -> 31 us  [on_device(): pl.pallas_call(functools.partial(kernel, n), out_shape=jax.ShapeDtypeStru...]
where the time goes in v2:
time: 32.5 us; the launch traced here: 32.3 us
  Pallas kernels  31 us (95%)
  local copies, waits for them, and re-layouts  1.28 us (4%)
    pallas_call x1, Pallas kernels, on_device(): pl.pallas_call(functools.partial(kernel, n), out_shape=jax.ShapeDtypeStru...  31 us
    unnamed x1, local copies, waits for them, and re-layouts  1.28 us

profile of v2, /device:TPU:0, one launch (start us, length us, event | category | flops | bytes accessed | tf_op | source)
XLA Modules:
  0.0 32.3 jit_solution(6851151643437564727)
XLA Ops:
  0.0 31.0 %shard_map.73 = bf16[4,4,128]{2,1,0:T(4,128)(2,1)} custom-call(bf16[4,4,128]{2,1,0:T(4,128)(2,1)} %q_hbm.1, bf16[64,4,128,128]{3,2,1,0:T(8,128)(2,1)} %k_hbm.1, bf16[64,4,128,128]{3,2,1,0:T(8,128)(2,1)} %v_hbm.1, bf16[32,4,128]{2,1,0:T(4,128)(2,1)} %kn_hbm.1, bf16[32,4,128]{2,1,0:T(4,128)(2,1)} %vn_hbm.1, s32[32]{0:T(128)} %len_hbm.1, s32[32,128]{1,0:T(8,128)} %bitcast.1), custom_call_target="tpu_custom_call" | custom-call | tf_op jit(solution)/shard_map/pallas_call | solution.py:282
  31.0 1.3 %copy.9 = bf16[4,4,128]{2,1,0:T(4,128)(2,1)} copy(bf16[4,4,128]{2,1,0:T(4,128)(2,1)} %shard_map.73) | data formatting | bytes 8192

commit v3 on v2

v3 whole, which is shorter than its diff:
```python
import functools
import math

import jax
import jax.numpy as jnp
from jax import lax
from jax.experimental import pallas as pl
from jax.experimental.pallas import tpu as pltpu
from jax.sharding import PartitionSpec as P

LOW = -1e30
FLOOR = -5e29
F32 = jnp.float32
BF16 = jnp.bfloat16


def hops(t):
    total = 0
    while t:
        total += (0, 1, 2, 1)[t % 4]
        t //= 4
    return total


def iota(shape, dim):
    return lax.broadcasted_iota(jnp.int32, shape, dim)


def dot(a, b, dims=((1,), (0,))):
    return lax.dot_general(a, b, (dims, ((), ())), preferred_element_type=F32)


def kernel(
    n, q_hbm, k_hbm, v_hbm, kn_hbm, vn_hbm, len_hbm, tbl_hbm, out_ref,
    q_ref, kn_ref, vn_ref, len_ref, tbl_ref,
    kbuf, vbuf, qall, racc, rml, sbuf, mine, sent, meta_v, meta_s,
    ksem, vsem, qsem, insem, lsem, msem, qs_sem, qr_sem, out_sem, in_sem,
):
    pages, heads, page_len, width = kbuf.shape
    seqs = len_ref.shape[0]
    slots = tbl_ref.shape[1]
    me = lax.axis_index("kv")
    head = lax.axis_index("head")
    c = math.log2(math.e) / math.sqrt(width)
    order = sorted(range(1, n), key=hops, reverse=True)

    def peer(t):
        return (jnp.bitwise_xor(me, t), head)

    barrier = pltpu.get_barrier_semaphore()
    for t in order:
        pl.semaphore_signal(barrier, inc=1, device_id=peer(t), device_id_type=pl.DeviceIdType.MESH)

    owned = me // 2
    q_copy = pltpu.make_async_copy(q_hbm, q_ref, qsem)
    q_copy.start()
    len_copy = pltpu.make_async_copy(len_hbm, len_ref, lsem)
    len_copy.start()
    small = [
        pltpu.make_async_copy(tbl_hbm, tbl_ref, insem.at[0]),
        pltpu.make_async_copy(kn_hbm.at[owned], kn_ref, insem.at[1]),
        pltpu.make_async_copy(vn_hbm.at[owned], vn_ref, insem.at[2]),
    ]
    for one in small:
        one.start()
    q_copy.wait()
    len_copy.wait()
    for one in small:
        one.wait()
    parts = 8
    step = pages // parts
    for hbm, buf, sem in ((k_hbm, kbuf, ksem), (v_hbm, vbuf, vsem)):
        for i in range(parts):
            pltpu.make_async_copy(hbm.at[pl.ds(i * step, step)], buf.at[pl.ds(i * step, step)], sem).start()

    q16 = q_ref[...].astype(F32).reshape(16, width)
    qall[me] = q16.astype(BF16)


    rel = tbl_ref[...] - me * pages
    here = jnp.logical_and(rel >= 0, rel < pages)
    here_f = jnp.where(here, 1.0, 0.0)
    here_b = here_f.astype(BF16)
    upper = jnp.where(iota((slots, slots), 0) < iota((slots, slots), 1), 1.0, 0.0).astype(BF16)
    ones = jnp.full((slots, slots), 1.0, BF16)
    lower = jnp.where(iota((seqs, seqs), 1) < iota((seqs, seqs), 0), 1.0, 0.0).astype(BF16)
    in_row = dot(here_b, upper)
    row_total = dot(here_b, ones)
    before = dot(lower, row_total.astype(BF16))
    place = jnp.where(here, in_row + before, -1.0)
    value = ((iota((seqs, slots), 0) * slots + iota((seqs, slots), 1)) * pages + rel).astype(F32)
    value = jnp.where(here, value, 0.0)
    kth = iota((pages, slots), 0).astype(F32)
    found = jnp.zeros((pages, slots), F32)
    for s in range(seqs):
        found = found + jnp.where(place[s : s + 1] == kth, value[s : s + 1], 0.0)
    found = jnp.sum(found, axis=1, keepdims=True)
    lane = iota((pages, slots), 1)
    row = jnp.sum(jnp.where(lane == iota((pages, slots), 0), found, 0.0), axis=0, keepdims=True)
    ends = before + row_total
    lane = iota((seqs, slots), 1)
    row = row + jnp.sum(jnp.where(lane == iota((seqs, slots), 0) + pages, ends, 0.0), axis=0, keepdims=True)
    meta_v[...] = row.astype(jnp.int32)
    copy = pltpu.make_async_copy(meta_v, meta_s, msem)
    copy.start()

    row_g = iota((16, width), 0) // 4
    kn = kn_ref[...].astype(F32)
    vn = vn_ref[...].astype(F32)
    kn16 = jnp.zeros((16, width), F32)
    vn16 = jnp.zeros((16, width), F32)
    for g in range(heads):
        kn16 = jnp.where(row_g == g, kn[g : g + 1], kn16)
        vn16 = jnp.where(row_g == g, vn[g : g + 1], vn16)
    new_raw = jnp.sum(q16 * kn16, axis=1, keepdims=True)

    copy.wait()

    pl.semaphore_wait(barrier, n - 1)
    for t in order:
        pltpu.make_async_remote_copy(
            src_ref=qall.at[me], dst_ref=qall.at[me], send_sem=qs_sem, recv_sem=qr_sem,
            device_id=peer(t), device_id_type=pl.DeviceIdType.MESH,
        ).start()

    pltpu.make_async_copy(k_hbm, kbuf, ksem).wait()
    pltpu.make_async_copy(v_hbm, vbuf, vsem).wait()
    pltpu.make_async_copy(qall.at[pl.ds(0, n - 1)], qall.at[pl.ds(0, n - 1)], qr_sem).wait()

    row_group = (iota((32, width), 0) // 4) % 4
    low_half = iota((16, page_len), 0) % 8 < 4
    lanes = iota((16, page_len), 1)
    chunk = sbuf.shape[0]
    page_bits = pages.bit_length() - 1
    slot_bits = slots.bit_length() - 1

    def decode(k):
        code = meta_s[0, k]
        slot = jnp.bitwise_and(code >> page_bits, slots - 1)
        seq = jnp.bitwise_and(code >> (page_bits + slot_bits), seqs - 1)
        return jnp.bitwise_and(code, pages - 1), seq, slot

    def scores(k, pair):
        lhs, rhs = [], []
        for at in (k, k + 1):
            p, s, _ = decode(at)
            qb = qall[pl.ds(2 * s, 2)].reshape(32, width)
            none = jnp.zeros_like(qb)
            lhs.append(
                jnp.concatenate([jnp.where(row_group == 2 * pair + u, qb, none) for u in range(2)], axis=1)
            )
            rhs.append(jnp.concatenate([kbuf[p, 2 * pair], kbuf[p, 2 * pair + 1]], axis=1))
        raw = dot(jnp.concatenate(lhs, axis=0), jnp.concatenate(rhs, axis=0), ((1,), (1,)))
        a, b = 8 * pair, 16 + 8 * pair
        return (
            jnp.concatenate([raw[a : a + 8, :page_len], raw[b : b + 8, :page_len]], axis=0),
            jnp.concatenate([raw[32 + a : 40 + a, page_len:], raw[32 + b : 40 + b, page_len:]], axis=0),
        )

    def attend(k, pair, raw, state):
        m, l, acc = state
        p, s, slot = decode(k)
        before_seq = decode(jnp.maximum(k - 1, 0))[1]
        first = jnp.logical_or(k == 0, before_seq != s)
        valid = len_ref[s] - 1 - slot * page_len
        raw = jnp.where(lanes < valid, raw, LOW)
        top = jnp.maximum(jnp.max(raw, axis=1, keepdims=True), FLOOR)
        weights = jnp.exp2((raw - top) * c)
        total = jnp.sum(weights, axis=1, keepdims=True)
        lhs = jnp.concatenate(
            [jnp.where(low_half, weights, 0.0).astype(BF16), jnp.where(low_half, 0.0, weights).astype(BF16)], axis=1
        )
        page_out = dot(lhs, vbuf[p, pl.ds(2 * pair, 2)].reshape(2 * page_len, width))
        top = jnp.broadcast_to(top, m.shape)
        m = jnp.where(first, FLOOR, m)
        new_m = jnp.maximum(m, top)
        old = jnp.where(first, 0.0, jnp.exp2((m - new_m) * c))
        new = jnp.exp2((top - new_m) * c)
        l = l * old + total * new
        acc = acc * old + page_out * new
        racc[k] = acc
        rml[k] = jnp.where(lanes < 64, new_m, l)
        return new_m, l, acc

    zero = jnp.zeros((16, width), F32)
    steps = pages // chunk
    lane8 = iota((8, width), 1) % 64
    left = iota((n, width), 1) < 64
    for pair in range(2):

        def fill(i):
            for u in range(0, chunk, 2):
                sbuf[u], sbuf[u + 1] = scores(i * chunk + u, pair)

        def body(i, state):
            raws = [sbuf[u] for u in range(chunk)]
            fill(i + 1)
            for u in range(chunk):
                state = attend(i * chunk + u, pair, raws[u], state)
            return state

        fill(0)
        state = lax.fori_loop(0, steps - 1, body, (zero, zero, zero))
        for u in range(chunk):
            state = attend((steps - 1) * chunk + u, pair, sbuf[u], state)

        def gather(s, stat):
            end = meta_s[0, pages + s]
            start = jnp.where(s == 0, 0, meta_s[0, pages + jnp.maximum(s - 1, 0)])
            some = end > start
            last = jnp.clip(end - 1, 0, pages - 1)
            acc = jnp.where(some, racc[last], 0.0)
            ml = jnp.where(some, rml[last], jnp.where(lanes < 64, FLOOR, 0.0))
            mine[pair, 2 * s, 0:8] = acc[:8]
            mine[pair, 2 * s + 1, 0:8] = acc[8:]
            stat = jnp.where(lane8 == 2 * s, ml[:8], stat)
            return jnp.where(lane8 == 2 * s + 1, ml[8:], stat)

        stat = lax.fori_loop(0, seqs, gather, jnp.zeros((8, width), F32), unroll=4)
        turned = jnp.concatenate([stat] * 16, axis=0).T
        mine[pair, :, 8, :] = jnp.where(left, turned[:n], turned[n:])
        for t in order:
            pltpu.make_async_remote_copy(
                src_ref=mine.at[pair, jnp.bitwise_xor(me, t)], dst_ref=sent.at[pair, me],
                send_sem=out_sem.at[pair], recv_sem=in_sem.at[pair],
                device_id=peer(t), device_id_type=pl.DeviceIdType.MESH,
            ).start()
        sent[pair, me] = mine[pair, me]

    at_row = iota((8, width), 1) % 8 == iota((8, width), 0)
    first8 = jnp.logical_and(at_row, iota((8, width), 1) < 8)
    in_block = iota((16, width), 1) // 8 == iota((16, width), 0)
    for pair in range(2):
        some = sent.at[pair, pl.ds(0, n - 1)]
        pltpu.make_async_copy(some, some, in_sem.at[pair]).wait()
        stats = sent[pair, :, 8, :]
        turned = pltpu.roll(stats, 64, axis=1)
        tops = jnp.where(left, stats, turned)
        top = jnp.max(tops, axis=0, keepdims=True)
        w = jnp.exp2((tops - top) * c)
        total = jnp.sum(w * turned, axis=0, keepdims=True)
        top8 = jnp.sum(jnp.where(first8, top, 0.0), axis=1, keepdims=True)
        sum8 = jnp.sum(jnp.where(first8, total, 0.0), axis=1, keepdims=True)
        blocks = []
        for b in range(n // 16):
            line = jnp.sum(jnp.where(in_block, w[16 * b : 16 * b + 16], 0.0), axis=0, keepdims=True)
            blocks.append(jnp.where(at_row, line, 0.0))
        wide = jnp.concatenate(blocks, axis=1)
        wide_hi = wide.astype(BF16).astype(F32)
        lhs = jnp.concatenate([wide_hi, wide - wide_hi], axis=0).astype(BF16)
        parts = sent[pair, :, 0:8, :].reshape(8 * n, width)
        parts_hi = parts.astype(BF16)
        parts_lo = (parts - parts_hi.astype(F32)).astype(BF16)
        both = dot(lhs, parts_hi)
        numer = both[:8] + both[8:] + dot(lhs, parts_lo)[:8]
        rows = slice(8 * pair, 8 * pair + 8)
        high = jnp.maximum(top8, new_raw[rows])
        old = jnp.exp2((top8 - high) * c)
        new = jnp.exp2((new_raw[rows] - high) * c)
        result = (numer * old + new * vn16[rows]) / (sum8 * old + new)
        out_ref[2 * pair : 2 * pair + 2] = result.reshape(2, 4, width).astype(BF16)

    some = qall.at[pl.ds(0, n - 1)]
    pltpu.make_async_copy(some, some, qs_sem).wait()
    for pair in range(2):
        some = mine.at[pair, pl.ds(0, n - 1)]
        pltpu.make_async_copy(some, some, out_sem.at[pair]).wait()


def on_device(queries, key_cache, value_cache, key_new, value_new, lengths, page_table):
    n = lax.axis_size("kv")
    heads, rows, width = queries.shape
    pages, _, page_len, _ = key_cache.shape
    seqs = lengths.shape[0]
    vmem = pl.BlockSpec(memory_space=pltpu.VMEM)
    hbm = pl.BlockSpec(memory_space=pltpu.HBM)
    dma = pltpu.SemaphoreType.DMA
    out = pl.pallas_call(
        functools.partial(kernel, n),
        out_shape=jax.ShapeDtypeStruct(queries.shape, BF16),
        in_specs=[hbm] * 7,
        out_specs=vmem,
        scratch_shapes=[
            pltpu.VMEM(queries.shape, BF16),
            pltpu.VMEM((heads, width), BF16),
            pltpu.VMEM((heads, width), BF16),
            pltpu.SMEM((seqs,), jnp.int32),
            pltpu.VMEM((seqs, page_table.shape[0] // seqs), jnp.int32),
            pltpu.VMEM(key_cache.shape, BF16),
            pltpu.VMEM(value_cache.shape, BF16),
            pltpu.VMEM((n, 16, width), BF16),
            pltpu.VMEM((pages, 16, width), F32),
            pltpu.VMEM((pages, 16, width), F32),
            pltpu.VMEM((16, 16, page_len), F32),
            pltpu.VMEM((2, n, 9, width), F32),
            pltpu.VMEM((2, n, 9, width), F32),
            pltpu.VMEM((1, width), jnp.int32),
            pltpu.SMEM((1, width), jnp.int32),
            dma,
            dma,
            dma,
            dma((3,)),
            *[dma] * 4,
            dma((2,)),
            dma((2,)),
        ],
        compiler_params=pltpu.CompilerParams(
            collective_id=0, has_side_effects=True
        ),
    )(queries, key_cache, value_cache, key_new, value_new, lengths, page_table.reshape(seqs, -1))
    return out


def solution(mesh):
    placed = (
        P("head", "kv", None),
        P("kv", "head", None, None),
        P("kv", "head", None, None),
        P(None, "head", None),
        P(None, "head", None),
        P(),
        P(),
    )
    return jax.shard_map(
        on_device, mesh=mesh, in_specs=placed, out_specs=P("head", "kv", None), check_vma=False
    )
```

time: 32.5 us -> 30.9 us (0.951)
  Pallas kernels: 31 us -> 29.5 us
    pallas_call x1, Pallas kernels: 31 us -> 29.5 us  [on_device(): pl.pallas_call(functools.partial(kernel, n), out_shape=jax.ShapeDtypeStru...]
where the time goes in v3:
time: 30.9 us; the launch traced here: 30.8 us
  Pallas kernels  29.5 us (95%)
  local copies, waits for them, and re-layouts  1.28 us (4%)
    pallas_call x1, Pallas kernels, on_device(): pl.pallas_call(functools.partial(kernel, n), out_shape=jax.ShapeDtypeStru...  29.5 us
    unnamed x1, local copies, waits for them, and re-layouts  1.28 us

profile of v3, /device:TPU:0, one launch (start us, length us, event | category | flops | bytes accessed | tf_op | source)
XLA Modules:
  0.0 30.8 jit_solution(1122247839238905801)
XLA Ops:
  0.0 29.5 %shard_map.73 = bf16[4,4,128]{2,1,0:T(4,128)(2,1)} custom-call(bf16[4,4,128]{2,1,0:T(4,128)(2,1)} %q_hbm.1, bf16[64,4,128,128]{3,2,1,0:T(8,128)(2,1)} %k_hbm.1, bf16[64,4,128,128]{3,2,1,0:T(8,128)(2,1)} %v_hbm.1, bf16[32,4,128]{2,1,0:T(4,128)(2,1)} %kn_hbm.1, bf16[32,4,128]{2,1,0:T(4,128)(2,1)} %vn_hbm.1, s32[32]{0:T(128)} %len_hbm.1, s32[32,128]{1,0:T(8,128)} %bitcast.1), custom_call_target="tpu_custom_call" | custom-call | tf_op jit(solution)/shard_map/pallas_call | solution.py:278
  29.5 1.3 %copy.9 = bf16[4,4,128]{2,1,0:T(4,128)(2,1)} copy(bf16[4,4,128]{2,1,0:T(4,128)(2,1)} %shard_map.73) | data formatting | bytes 8192

commit v4 on v3

--- a/solution.py
+++ b/solution.py
@@ -258,7 +258,7 @@
         old = jnp.exp2((top8 - high) * c)
         new = jnp.exp2((new_raw[rows] - high) * c)
         result = (numer * old + new * vn16[rows]) / (sum8 * old + new)
-        out_ref[2 * pair : 2 * pair + 2] = result.reshape(2, 4, width).astype(BF16)
+        out_ref[rows] = result
 
     some = qall.at[pl.ds(0, n - 1)]
     pltpu.make_async_copy(some, some, qs_sem).wait()
@@ -275,9 +275,10 @@
     vmem = pl.BlockSpec(memory_space=pltpu.VMEM)
     hbm = pl.BlockSpec(memory_space=pltpu.HBM)
     dma = pltpu.SemaphoreType.DMA
+    inputs = (queries, key_cache, value_cache, key_new, value_new, lengths, page_table.reshape(seqs, -1))
     out = pl.pallas_call(
         functools.partial(kernel, n),
-        out_shape=jax.ShapeDtypeStruct(queries.shape, BF16),
+        out_shape=jax.ShapeDtypeStruct((heads * rows, width), F32),
         in_specs=[hbm] * 7,
         out_specs=vmem,
         scratch_shapes=[
@@ -305,10 +306,10 @@
             dma((2,)),
         ],
         compiler_params=pltpu.CompilerParams(
-            collective_id=0, has_side_effects=True
+            collective_id=0, has_side_effects=True, vmem_limit_bytes=48 * 1024 * 1024
         ),
-    )(queries, key_cache, value_cache, key_new, value_new, lengths, page_table.reshape(seqs, -1))
-    return out
+    )(*(pltpu.with_memory_space_constraint(x, pltpu.HBM) for x in inputs))
+    return out.reshape(heads, rows, width).astype(BF16)
 
 
 def solution(mesh):

time: 30.9 us -> 29.7 us (0.961)
  local copies, waits for them, and re-layouts: 1.28 us -> 0 us
  Pallas kernels: 29.5 us -> 28.9 us
  other arithmetic: 0 us -> 0.6 us
    unnamed x1 -> x0, local copies, waits for them, and re-layouts: 1.28 us -> none
    convert_element_type x0 -> x1, other arithmetic: none -> 0.6 us  [on_device(): return out.reshape(heads, rows, width).astype(BF16)]
    pallas_call x1, Pallas kernels: 29.5 us -> 28.9 us  [on_device(): pl.pallas_call(functools.partial(kernel, n), out_shape=jax.ShapeDtypeStru...]
where the time goes in v4:
time: 29.7 us; the launch traced here: 29.5 us
  Pallas kernels  28.9 us (97%)
  other arithmetic  0.6 us (2%)
    pallas_call x1, Pallas kernels, on_device(): pl.pallas_call(functools.partial(kernel, n), out_shape=jax.ShapeDtypeStru...  28.9 us
    convert_element_type x1, other arithmetic, on_device(): return out.reshape(heads, rows, width).astype(BF16)  0.6 us

profile of v4, /device:TPU:0, one launch (start us, length us, event | category | flops | bytes accessed | tf_op | source)
XLA Modules:
  0.0 29.5 jit_solution(9666198555415129822)
XLA Ops:
  0.0 28.9 %shard_map.73 = f32[16,128]{1,0:T(8,128)S(1)} custom-call(bf16[4,4,128]{2,1,0:T(4,128)(2,1)} %q_hbm.1, bf16[64,4,128,128]{3,2,1,0:T(8,128)(2,1)} %k_hbm.1, bf16[64,4,128,128]{3,2,1,0:T(8,128)(2,1)} %v_hbm.1, bf16[32,4,128]{2,1,0:T(4,128)(2,1)} %kn_hbm.1, bf16[32,4,128]{2,1,0:T(4,128)(2,1)} %vn_hbm.1, s32[32]{0:T(128)} %len_hbm.1, s32[32,128]{1,0:T(8,128)} %bitcast.2), custom_call_target="tpu_custom_call" | custom-call | tf_op jit(solution)/shard_map/pallas_call | solution.py:279
  28.9 0.6 %convert_element_type.6 = bf16[16,128]{1,0:T(8,128)(2,1)} convert(f32[16,128]{1,0:T(8,128)S(1)} %shard_map.73) | non-fusion elementwise | flops 2048 | bytes 12288 | tf_op jit(solution)/shard_map/convert_element_type | solution.py:312

commit v5 on v4

--- a/solution.py
+++ b/solution.py
@@ -8,6 +8,7 @@
 from jax.experimental.pallas import tpu as pltpu
 from jax.sharding import PartitionSpec as P
 
+UNROLL = 4
 LOW = -1e30
 FLOOR = -5e29
 F32 = jnp.float32
@@ -124,6 +125,13 @@
         ).start()
 
     pltpu.make_async_copy(k_hbm, kbuf, ksem).wait()
+
+    def turn(p, carry):
+        for g in range(heads):
+            kbuf[p, g] = kbuf[p, g].T
+        return carry
+
+    lax.fori_loop(0, pages, turn, 0, unroll=UNROLL)
     pltpu.make_async_copy(v_hbm, vbuf, vsem).wait()
     pltpu.make_async_copy(qall.at[pl.ds(0, n - 1)], qall.at[pl.ds(0, n - 1)], qr_sem).wait()
 
@@ -149,8 +157,8 @@
             lhs.append(
                 jnp.concatenate([jnp.where(row_group == 2 * pair + u, qb, none) for u in range(2)], axis=1)
             )
-            rhs.append(jnp.concatenate([kbuf[p, 2 * pair], kbuf[p, 2 * pair + 1]], axis=1))
-        raw = dot(jnp.concatenate(lhs, axis=0), jnp.concatenate(rhs, axis=0), ((1,), (1,)))
+            rhs.append(kbuf[p, pl.ds(2 * pair, 2)].reshape(2 * width, page_len))
+        raw = dot(jnp.concatenate(lhs, axis=0), jnp.concatenate(rhs, axis=1))
         a, b = 8 * pair, 16 + 8 * pair
         return (
             jnp.concatenate([raw[a : a + 8, :page_len], raw[b : b + 8, :page_len]], axis=0),
@@ -292,7 +300,7 @@
             pltpu.VMEM((n, 16, width), BF16),
             pltpu.VMEM((pages, 16, width), F32),
             pltpu.VMEM((pages, 16, width), F32),
-            pltpu.VMEM((16, 16, page_len), F32),
+            pltpu.VMEM((32, 16, page_len), F32),
             pltpu.VMEM((2, n, 9, width), F32),
             pltpu.VMEM((2, n, 9, width), F32),
             pltpu.VMEM((1, width), jnp.int32),

time: 29.7 us -> 28.6 us (0.963)
  Pallas kernels: 28.9 us -> 27.8 us
    pallas_call x1, Pallas kernels: 28.9 us -> 27.8 us  [on_device(): pl.pallas_call(functools.partial(kernel, n), out_shape=jax.ShapeDtypeStru...]
where the time goes in v5:
time: 28.6 us; the launch traced here: 28.4 us
  Pallas kernels  27.8 us (97%)
  other arithmetic  0.6 us (2%)
    pallas_call x1, Pallas kernels, on_device(): pl.pallas_call(functools.partial(kernel, n), out_shape=jax.ShapeDtypeStru...  27.8 us
    convert_element_type x1, other arithmetic, on_device(): return out.reshape(heads, rows, width).astype(BF16)  0.6 us

profile of v5, /device:TPU:0, one launch (start us, length us, event | category | flops | bytes accessed | tf_op | source)
XLA Modules:
  0.0 28.4 jit_solution(16337679465109830817)
XLA Ops:
  0.0 27.8 %shard_map.73 = f32[16,128]{1,0:T(8,128)S(1)} custom-call(bf16[4,4,128]{2,1,0:T(4,128)(2,1)} %q_hbm.1, bf16[64,4,128,128]{3,2,1,0:T(8,128)(2,1)} %k_hbm.1, bf16[64,4,128,128]{3,2,1,0:T(8,128)(2,1)} %v_hbm.1, bf16[32,4,128]{2,1,0:T(4,128)(2,1)} %kn_hbm.1, bf16[32,4,128]{2,1,0:T(4,128)(2,1)} %vn_hbm.1, s32[32]{0:T(128)} %len_hbm.1, s32[32,128]{1,0:T(8,128)} %bitcast.2), custom_call_target="tpu_custom_call" | custom-call | tf_op jit(solution)/shard_map/pallas_call | solution.py:287
  27.9 0.6 %convert_element_type.6 = bf16[16,128]{1,0:T(8,128)(2,1)} convert(f32[16,128]{1,0:T(8,128)S(1)} %shard_map.73) | non-fusion elementwise | flops 2048 | bytes 12288 | tf_op jit(solution)/shard_map/convert_element_type | solution.py:320

commit v6 on v5

--- a/solution.py
+++ b/solution.py
@@ -196,21 +196,16 @@
     left = iota((n, width), 1) < 64
     for pair in range(2):
 
-        def fill(i):
-            for u in range(0, chunk, 2):
-                sbuf[u], sbuf[u + 1] = scores(i * chunk + u, pair)
-
-        def body(i, state):
-            raws = [sbuf[u] for u in range(chunk)]
-            fill(i + 1)
-            for u in range(chunk):
-                state = attend(i * chunk + u, pair, raws[u], state)
-            return state
-
-        fill(0)
-        state = lax.fori_loop(0, steps - 1, body, (zero, zero, zero))
-        for u in range(chunk):
-            state = attend((steps - 1) * chunk + u, pair, sbuf[u], state)
+        ahead = 8
+        raws = {}
+        state = (zero, zero, zero)
+        for k in range(0, ahead, 2):
+            raws[k], raws[k + 1] = scores(k, pair)
+        for k in range(0, pages, 2):
+            if k + ahead < pages:
+                raws[k + ahead], raws[k + ahead + 1] = scores(k + ahead, pair)
+            for u in (k, k + 1):
+                state = attend(u, pair, raws.pop(u), state)
 
         def gather(s, stat):
             end = meta_s[0, pages + s]

time: 28.6 us -> 28.6 us (level)
  no operation moved by 1% of the time
where the time goes in v6:
time: 28.6 us; the launch traced here: 28.5 us
  Pallas kernels  27.9 us (98%)
  other arithmetic  0.6 us (2%)
    pallas_call x1, Pallas kernels, on_device(): pl.pallas_call(functools.partial(kernel, n), out_shape=jax.ShapeDtypeStru...  27.9 us
    convert_element_type x1, other arithmetic, on_device(): return out.reshape(heads, rows, width).astype(BF16)  0.6 us

profile of v6, /device:TPU:0, one launch (start us, length us, event | category | flops | bytes accessed | tf_op | source)
XLA Modules:
  0.0 28.5 jit_solution(3440473802756123582)
XLA Ops:
  0.0 27.9 %shard_map.73 = f32[16,128]{1,0:T(8,128)S(1)} custom-call(bf16[4,4,128]{2,1,0:T(4,128)(2,1)} %q_hbm.1, bf16[64,4,128,128]{3,2,1,0:T(8,128)(2,1)} %k_hbm.1, bf16[64,4,128,128]{3,2,1,0:T(8,128)(2,1)} %v_hbm.1, bf16[32,4,128]{2,1,0:T(4,128)(2,1)} %kn_hbm.1, bf16[32,4,128]{2,1,0:T(4,128)(2,1)} %vn_hbm.1, s32[32]{0:T(128)} %len_hbm.1, s32[32,128]{1,0:T(8,128)} %bitcast.2), custom_call_target="tpu_custom_call" | custom-call | tf_op jit(solution)/shard_map/pallas_call | solution.py:282
  27.9 0.6 %convert_element_type.6 = bf16[16,128]{1,0:T(8,128)(2,1)} convert(f32[16,128]{1,0:T(8,128)S(1)} %shard_map.73) | non-fusion elementwise | flops 2048 | bytes 12288 | tf_op jit(solution)/shard_map/convert_element_type | solution.py:315
